TPU v7x, 32 devices: a whole 2x2x4 slice. The times are simulated.
32 devices in a mesh: blk: 8 (over y, x, core), col: 4 (over z).
Axes of the slice: x: 2, y: 2, z: 4, core: 2. Of those that a mesh axis runs over, the one named last changes fastest.
Arguments:
- samples: bfloat16 [2048, 768], P('blk'), may hold values from -3 to 3
- targets: float32 [2048, 256], P('blk'), may hold values from -6 to 6
- batch_index: int32 [1024], P('blk'), may hold values from 0 to 255
- centers: bfloat16 [4096, 768], P(('blk', 'col')), may hold values from -3 to 3
- weights: float32 [4096, 256], P(('blk', 'col')), may hold values from -6 to 6
- nystrom_index: int32 [1536], replicated, may hold values from 0 to 4095, as said below
- eigvecs: float32 [1536, 128], replicated, may hold values from -0.15625 to 0.15625
- coefficient: float32 [128], replicated, may hold values from 0.4 to 0.95
Outputs:
- residual: float32 [1024, 256], P(('blk', 'col'))
- new_weights: float32 [4096, 256], P(('blk', 'col'))
Inputs may be any that keep to these rules, and one draw needn't show every extreme that they name: Batch row i is sample row (i // 128) * 256 + batch_index[i]. `nystrom_index`: 1536 distinct center rows.
All inputs are finite; a program needn't handle non-finite values.
Results may differ from a plain program's by a relative error of at most 0.0003.
The roundings to bfloat16 on the way count: a program that leaves them out, or rounds other values in their place, can miss the bound.
Values may be sent and summed in bfloat16 or wider, within the bound.
No kernel may reach another device: no remote copies, remote signals or barrier semaphores. Data moves between devices by JAX's collectives and lax.ppermute only.
A program may use at most 64 MiB of HBM per device.

v0:
```python
import jax
import jax.numpy as jnp
from jax import lax
from jax.sharding import PartitionSpec as P

spread = 1.0
shift_sq = 1.0
step_size = 4.0


def shifted(block, axis, distance):
    devices = range(lax.axis_size(axis))
    route = [((i - distance) % len(devices), i) for i in devices]
    return lax.ppermute(block, axis, route)


def kernel_block(points, centers, center_sq):
    point_sq = jnp.sum(jnp.square(points.astype(jnp.float32)), axis=1, keepdims=True)
    cross = lax.dot_general(
        points, centers, (((1,), (1,)), ((), ())), preferred_element_type=jnp.float32
    )
    dist_sq = point_sq + center_sq[None, :] - 2.0 * cross
    return jnp.exp(-jnp.sqrt(dist_sq + shift_sq) / spread).astype(jnp.bfloat16)


def move_up(points_now):
    return shifted(points_now, "blk", 1)


def pass_up(partial_value):
    return shifted(partial_value, "blk", 1)


def local(samples, targets, batch_index, centers, weights, nystrom_index, eigvecs, coefficient):
    blocks = lax.axis_size("blk")
    columns = lax.axis_size("col")
    my_block = lax.axis_index("blk")
    blk_rows = batch_index.shape[0]
    n_center = centers.shape[0]
    out_width = weights.shape[1]
    points = jnp.take(samples, batch_index, axis=0)
    wanted = jnp.take(targets, batch_index, axis=0)
    center_sq = jnp.sum(jnp.square(centers.astype(jnp.float32)), axis=1)
    weights_low = weights.astype(jnp.bfloat16)
    kernel_store = jnp.zeros((blocks * blk_rows, n_center), jnp.bfloat16)

    def absorb(points_now, partial_value, stored, offset):
        kernel = kernel_block(points_now, centers, center_sq)
        stored = lax.dynamic_update_slice(stored, kernel, (offset, 0))
        return (
            partial_value + jnp.dot(kernel, weights_low, preferred_element_type=jnp.float32),
            stored,
        )

    def walk_step(step_idx, state_now):
        points_now, partial_value, stored = state_now
        partial_value, stored = absorb(
            points_now, partial_value, stored, (my_block - step_idx) % blocks * blk_rows
        )
        return (move_up(points_now), pass_up(partial_value), stored)

    initial = (points, jnp.zeros((blk_rows, out_width), jnp.float32), kernel_store)
    points_now, partial_value, kernel_store = lax.fori_loop(0, blocks - 1, walk_step, initial)
    partial_value, kernel_store = absorb(
        points_now, partial_value, kernel_store, (my_block + 1) % blocks * blk_rows
    )
    partial_value = pass_up(partial_value)
    share_rows = blk_rows // columns
    prediction = lax.psum(partial_value, "col")
    residual_full = prediction - wanted
    gathered = lax.all_gather(residual_full.astype(jnp.bfloat16), "blk", axis=0, tiled=True)
    own_resid = lax.dynamic_slice_in_dim(
        residual_full, lax.axis_index("col") * share_rows, share_rows, 0
    )
    gradient = lax.dot_general(
        kernel_store, gathered, (((0,), (0,)), ((), ())), preferred_element_type=jnp.float32
    )
    first_row = lax.axis_index(("blk", "col")) * n_center
    position = nystrom_index - first_row
    inside = (position >= 0) & (position < n_center)
    position = jnp.where(inside, position, n_center)
    target_row = jnp.minimum(position, n_center - 1)
    picked = jnp.where(inside[:, None], jnp.take(gradient, target_row, axis=0), 0.0)
    highest = lax.Precision.HIGHEST
    local_proj = lax.dot_general(eigvecs, picked, (((0,), (0,)), ((), ())), precision=highest)
    projected = lax.psum(local_proj, ("blk", "col"))
    correction = jnp.dot(eigvecs, coefficient[:, None] * projected, precision=highest)
    adjusted = gradient.at[position].add(-correction, mode="drop")
    return (own_resid, weights - step_size * adjusted)


def solution(mesh):
    in_specs = (
        P("blk", None),
        P("blk", None),
        P("blk"),
        P(("blk", "col"), None),
        P(("blk", "col"), None),
        P(),
        P(),
        P(),
    )
    out_specs = (P(("blk", "col"), None), P(("blk", "col"), None))
    return jax.shard_map(local, mesh=mesh, in_specs=in_specs, out_specs=out_specs, check_vma=False)
```

profile of v0, /device:TPU:0, one launch (start us, length us, event | category | flops | bytes accessed | tf_op | source)
XLA Modules:
  0.0 271.0 jit_solution(4618817647422644272)
XLA Ops:
  7.2 0.8 compare_and_fusion.2
  8.0 0.7 compare_select_fusion.2
  8.7 1.0 multiply_reduce_fusion.2
  9.7 0.9 convert_element_type.36
  10.6 2.0 gather_fusion
  12.8 53.1 %while.19 = (s32[]{:T(128)}, bf16[128,768]{1,0:T(8,128)(2,1)S(1)}, f32[128,256]{1,0:T(8,128)S(1)}, bf16[1024,128]{1,0:T(8,128)(2,1)S(1)}, f32[128]{0:T(128)S(1)}...) while((s32[]{:T(128)}, bf16[128,768]{1,0:T(8,128)(2,1)S(1)}, ...), condition=%wide.region_3.4_spmd, body=%wide.region_1.3_spmd.sunk | while | flops 33980304 | bytes 2721664 | solution.py:63
  12.9 0.5 collective-permute-start
  13.5 0.3 constant_dynamic-update-slice_fusion.3
  13.8 0.2 convolution_add_fusion.3
  14.0 2.6 collective-permute-start.1
  16.6 4.4 %collective-permute-done.1 = f32[128,256]{1,0:T(8,128)S(1)} collective-permute-done((f32[128,256]{1,0:T(8,128)S(1)}, f32[128,256]{1,0:T(8,128)S(1)}, u32[]{:S(2)}, u32[]{:S(2)}) %collective-permute-start.1) | collective-permute-done | bytes 131104 | tf_op jit(solution)/shard_map/while/body/eval_jaxpr/ppermute | solution.py:14
  21.3 0.3 constant_dynamic-update-slice_fusion.3
  21.5 0.2 convolution_add_fusion.3
  21.7 1.5 collective-permute-start.1
  23.2 5.3 %collective-permute-done.1 = f32[128,256]{1,0:T(8,128)S(1)} collective-permute-done((f32[128,256]{1,0:T(8,128)S(1)}, f32[128,256]{1,0:T(8,128)S(1)}, u32[]{:S(2)}, u32[]{:S(2)}) %collective-permute-start.1) | collective-permute-done | bytes 131104 | tf_op jit(solution)/shard_map/while/body/eval_jaxpr/ppermute | solution.py:14
  28.8 0.3 constant_dynamic-update-slice_fusion.3
  29.0 0.2 convolution_add_fusion.3
  29.2 0.6 collective-permute-start.1
  29.7 6.2 %collective-permute-done.1 = f32[128,256]{1,0:T(8,128)S(1)} collective-permute-done((f32[128,256]{1,0:T(8,128)S(1)}, f32[128,256]{1,0:T(8,128)S(1)}, u32[]{:S(2)}, u32[]{:S(2)}) %collective-permute-start.1) | collective-permute-done | bytes 131104 | tf_op jit(solution)/shard_map/while/body/eval_jaxpr/ppermute | solution.py:14
  36.2 0.3 constant_dynamic-update-slice_fusion.3
  36.5 0.2 convolution_add_fusion.3
  36.7 6.8 %collective-permute-done.1 = f32[128,256]{1,0:T(8,128)S(1)} collective-permute-done((f32[128,256]{1,0:T(8,128)S(1)}, f32[128,256]{1,0:T(8,128)S(1)}, u32[]{:S(2)}, u32[]{:S(2)}) %collective-permute-start.1) | collective-permute-done | bytes 131104 | tf_op jit(solution)/shard_map/while/body/eval_jaxpr/ppermute | solution.py:14
  43.7 0.3 constant_dynamic-update-slice_fusion.3
  44.0 0.2 convolution_add_fusion.3
  44.2 6.8 %collective-permute-done.1 = f32[128,256]{1,0:T(8,128)S(1)} collective-permute-done((f32[128,256]{1,0:T(8,128)S(1)}, f32[128,256]{1,0:T(8,128)S(1)}, u32[]{:S(2)}, u32[]{:S(2)}) %collective-permute-start.1) | collective-permute-done | bytes 131104 | tf_op jit(solution)/shard_map/while/body/eval_jaxpr/ppermute | solution.py:14
  51.2 0.3 constant_dynamic-update-slice_fusion.3
  51.4 0.2 convolution_add_fusion.3
  51.7 6.8 %collective-permute-done.1 = f32[128,256]{1,0:T(8,128)S(1)} collective-permute-done((f32[128,256]{1,0:T(8,128)S(1)}, f32[128,256]{1,0:T(8,128)S(1)}, u32[]{:S(2)}, u32[]{:S(2)}) %collective-permute-start.1) | collective-permute-done | bytes 131104 | tf_op jit(solution)/shard_map/while/body/eval_jaxpr/ppermute | solution.py:14
  58.6 0.3 constant_dynamic-update-slice_fusion.3
  58.9 0.2 convolution_add_fusion.3
  59.1 6.8 %collective-permute-done.1 = f32[128,256]{1,0:T(8,128)S(1)} collective-permute-done((f32[128,256]{1,0:T(8,128)S(1)}, f32[128,256]{1,0:T(8,128)S(1)}, u32[]{:S(2)}, u32[]{:S(2)}) %collective-permute-start.1) | collective-permute-done | bytes 131104 | tf_op jit(solution)/shard_map/while/body/eval_jaxpr/ppermute | solution.py:14
  66.0 0.3 constant_dynamic-update-slice_fusion.1
  66.3 0.2 convolution_add_fusion.1
  66.5 5.2 %collective-permute-done.2 = f32[128,256]{1,0:T(8,128)S(1)} collective-permute-done((f32[128,256]{1,0:T(8,128)S(1)}, f32[128,256]{1,0:T(8,128)S(1)}, u32[]{:S(2)}, u32[]{:S(2)}) %collective-permute-start.2) | collective-permute-done | bytes 131104 | tf_op jit(solution)/shard_map/ppermute | solution.py:14
  71.8 0.7 copy-done.4
  72.5 0.8 gather_fusion.1
  73.3 35.0 %all-reduce.3.cloned.1.call-done = f32[128,256]{1,0:T(8,128)} async-done(((f32[128,256]{1,0:T(8,128)}), f32[128,256]{1,0:T(8,128)}) %all-reduce.3.cloned.1.call-update) | async-done | bytes 131088 | tf_op jit(solution)/shard_map/psum | solution.py:69
  108.3 1.0 fusion.27
  109.3 9.8 %all_gather.3 = bf16[1024,256]{1,0:T(8,128)(2,1)S(1)} all-gather(bf16[128,256]{1,0:T(8,128)(2,1)S(1)} %get-tuple-element.224), channel_id=1, replica_groups=mesh['blk'=8,'col'=4] {'blk'}, dimensions={0}, use_global_device_ids=true | all-gather | bytes 589824 | tf_op jit(solution)/shard_map/all_gather | solution.py:71
  119.1 0.3 fusion.28
  119.4 3.7 %gather_fusion.2 = f32[1536,256]{1,0:T(8,128)S(1)} fusion(f32[128,256]{1,0:T(8,128)S(1)} %fusion.28, s32[2048]{0:T(1024)S(1)} %pad_clamp_fusion), kind=kCustom, calls=%fused_computation.2 | custom fusion | bytes 3151872 | tf_op jit(solution)/shard_map/jit(_take)/gather | solution.py:83
  123.1 2.6 fusion.10
  125.7 0.6 constant_dynamic-slice_fusion
  126.3 122.8 %all-reduce.5.cloned.1.call-done = f32[128,256]{1,0:T(8,128)} async-done(((f32[128,256]{1,0:T(8,128)}), f32[128,256]{1,0:T(8,128)}) %all-reduce.5.cloned.1.call-update) | async-done | bytes 131088 | tf_op jit(solution)/shard_map/psum | solution.py:86
  249.1 3.6 %fusion.6 = f32[1536,256]{0,1:T(8,128)} fusion(f32[1536,128]{1,0:T(8,128)S(1)} %copy-done, f32[128,256]{1,0:T(8,128)} %all-reduce.5.cloned.1.call-done, f32[128]{0:T(128)S(1)} %copy-done.6), kind=kOutput, calls=%fused_computation.15 | convolution fusion | flops 604405760 | bytes 2490880 | tf_op jit(solution)/shard_map/dot_general | solution.py:87
  252.7 1.9 copy.10
  254.6 8.9 %scatter_fusion = f32[128,256]{1,0:T(8,128)S(1)} fusion(f32[128,256]{1,0:T(8,128)S(1)} %fusion.28, s32[1536]{0:T(1024)S(1)} %compare_select_fusion.1, f32[1536,256]{1,0:T(8,128)S(1)} %copy.10), kind=kCustom, calls=%fused_computation.3 | custom fusion | flops 393216 | bytes 4724736 | tf_op jit(solution)/shard_map/scatter-add | solution.py:88
  263.5 0.7 multiply_subtract_fusion
  (57 shorter events, 2.0 us)
Async XLA Ops:
  7.2 115.9 %copy-start = (f32[1536,128]{1,0:T(8,128)S(1)}, f32[1536,128]{1,0:T(8,128)}, u32[]{:S(2)}) copy-start(f32[1536,128]{1,0:T(8,128)} %param.16) | copy-start | bytes 2359300
  7.2 5.6 %copy-start.3 = (bf16[128,768]{1,0:T(8,128)(2,1)S(1)}, bf16[128,768]{1,0:T(8,128)(2,1)}, u32[]{:S(2)}) copy-start(bf16[128,768]{1,0:T(8,128)(2,1)} %param.13) | copy-start | bytes 589828
  7.2 101.1 %all-reduce.3.cloned.1.call-start = ((), (), s32[]{:S(2)}) async-start(), calls=%async_computation | async-start | bytes 262144 | tf_op jit(solution)/shard_map/psum | solution.py:69
  12.8 53.7 %copy-start.5 = (s32[1536]{0:T(1024)S(1)}, s32[1536]{0:T(1024)}, u32[]{:S(2)}) copy-start(s32[1536]{0:T(1024)} %param.15) | copy-start | bytes 18436
  12.9 8.2 %collective-permute-start = (bf16[128,768]{1,0:T(8,128)(2,1)S(1)}, bf16[128,768]{1,0:T(8,128)(2,1)S(1)}, u32[]{:S(2)}, u32[]{:S(2)}) collective-permute-start(bf16[128,768]{1,0:T(8,128)(2,1)S(1)} %copy.17), channel_id=1, source_target_pairs={{28,0},{0,4},{4,8},{8,12},{12,16},{16,20},{20,24},{24,28},{29,1},{... | collective-permute-start | bytes 589832 | tf_op jit(solution)/shard_map/while/body/eval_jaxpr/ppermute | solution.py:14
  14.0 7.1 %collective-permute-start.1 = (f32[128,256]{1,0:T(8,128)S(1)}, f32[128,256]{1,0:T(8,128)S(1)}, u32[]{:S(2)}, u32[]{:S(2)}) collective-permute-start(f32[128,256]{1,0:T(8,128)S(1)} %convolution_add_fusion.3), channel_id=1, source_target_pairs={{28,0},{0,4},{4,8},{8,12},{12,16},{16,20},{20,24},{24,28},{29,1},{... | collective-permute-start | bytes 393224 | tf_op jit(solution)/shard_map/while/body/eval_jaxpr/ppermute | solution.py:14
  21.1 7.5 %collective-permute-start = (bf16[128,768]{1,0:T(8,128)(2,1)S(1)}, bf16[128,768]{1,0:T(8,128)(2,1)S(1)}, u32[]{:S(2)}, u32[]{:S(2)}) collective-permute-start(bf16[128,768]{1,0:T(8,128)(2,1)S(1)} %copy.17), channel_id=1, source_target_pairs={{28,0},{0,4},{4,8},{8,12},{12,16},{16,20},{20,24},{24,28},{29,1},{... | collective-permute-start | bytes 589832 | tf_op jit(solution)/shard_map/while/body/eval_jaxpr/ppermute | solution.py:14
  21.7 6.8 %collective-permute-start.1 = (f32[128,256]{1,0:T(8,128)S(1)}, f32[128,256]{1,0:T(8,128)S(1)}, u32[]{:S(2)}, u32[]{:S(2)}) collective-permute-start(f32[128,256]{1,0:T(8,128)S(1)} %convolution_add_fusion.3), channel_id=1, source_target_pairs={{28,0},{0,4},{4,8},{8,12},{12,16},{16,20},{20,24},{24,28},{29,1},{... | collective-permute-start | bytes 393224 | tf_op jit(solution)/shard_map/while/body/eval_jaxpr/ppermute | solution.py:14
  28.5 7.5 %collective-permute-start = (bf16[128,768]{1,0:T(8,128)(2,1)S(1)}, bf16[128,768]{1,0:T(8,128)(2,1)S(1)}, u32[]{:S(2)}, u32[]{:S(2)}) collective-permute-start(bf16[128,768]{1,0:T(8,128)(2,1)S(1)} %copy.17), channel_id=1, source_target_pairs={{28,0},{0,4},{4,8},{8,12},{12,16},{16,20},{20,24},{24,28},{29,1},{... | collective-permute-start | bytes 589832 | tf_op jit(solution)/shard_map/while/body/eval_jaxpr/ppermute | solution.py:14
  29.2 6.8 %collective-permute-start.1 = (f32[128,256]{1,0:T(8,128)S(1)}, f32[128,256]{1,0:T(8,128)S(1)}, u32[]{:S(2)}, u32[]{:S(2)}) collective-permute-start(f32[128,256]{1,0:T(8,128)S(1)} %convolution_add_fusion.3), channel_id=1, source_target_pairs={{28,0},{0,4},{4,8},{8,12},{12,16},{16,20},{20,24},{24,28},{29,1},{... | collective-permute-start | bytes 393224 | tf_op jit(solution)/shard_map/while/body/eval_jaxpr/ppermute | solution.py:14
  36.0 7.5 %collective-permute-start = (bf16[128,768]{1,0:T(8,128)(2,1)S(1)}, bf16[128,768]{1,0:T(8,128)(2,1)S(1)}, u32[]{:S(2)}, u32[]{:S(2)}) collective-permute-start(bf16[128,768]{1,0:T(8,128)(2,1)S(1)} %copy.17), channel_id=1, source_target_pairs={{28,0},{0,4},{4,8},{8,12},{12,16},{16,20},{20,24},{24,28},{29,1},{... | collective-permute-start | bytes 589832 | tf_op jit(solution)/shard_map/while/body/eval_jaxpr/ppermute | solution.py:14
  36.6 6.8 %collective-permute-start.1 = (f32[128,256]{1,0:T(8,128)S(1)}, f32[128,256]{1,0:T(8,128)S(1)}, u32[]{:S(2)}, u32[]{:S(2)}) collective-permute-start(f32[128,256]{1,0:T(8,128)S(1)} %convolution_add_fusion.3), channel_id=1, source_target_pairs={{28,0},{0,4},{4,8},{8,12},{12,16},{16,20},{20,24},{24,28},{29,1},{... | collective-permute-start | bytes 393224 | tf_op jit(solution)/shard_map/while/body/eval_jaxpr/ppermute | solution.py:14
  43.5 7.5 %collective-permute-start = (bf16[128,768]{1,0:T(8,128)(2,1)S(1)}, bf16[128,768]{1,0:T(8,128)(2,1)S(1)}, u32[]{:S(2)}, u32[]{:S(2)}) collective-permute-start(bf16[128,768]{1,0:T(8,128)(2,1)S(1)} %copy.17), channel_id=1, source_target_pairs={{28,0},{0,4},{4,8},{8,12},{12,16},{16,20},{20,24},{24,28},{29,1},{... | collective-permute-start | bytes 589832 | tf_op jit(solution)/shard_map/while/body/eval_jaxpr/ppermute | solution.py:14
  44.1 6.8 %collective-permute-start.1 = (f32[128,256]{1,0:T(8,128)S(1)}, f32[128,256]{1,0:T(8,128)S(1)}, u32[]{:S(2)}, u32[]{:S(2)}) collective-permute-start(f32[128,256]{1,0:T(8,128)S(1)} %convolution_add_fusion.3), channel_id=1, source_target_pairs={{28,0},{0,4},{4,8},{8,12},{12,16},{16,20},{20,24},{24,28},{29,1},{... | collective-permute-start | bytes 393224 | tf_op jit(solution)/shard_map/while/body/eval_jaxpr/ppermute | solution.py:14
  51.0 7.5 %collective-permute-start = (bf16[128,768]{1,0:T(8,128)(2,1)S(1)}, bf16[128,768]{1,0:T(8,128)(2,1)S(1)}, u32[]{:S(2)}, u32[]{:S(2)}) collective-permute-start(bf16[128,768]{1,0:T(8,128)(2,1)S(1)} %copy.17), channel_id=1, source_target_pairs={{28,0},{0,4},{4,8},{8,12},{12,16},{16,20},{20,24},{24,28},{29,1},{... | collective-permute-start | bytes 589832 | tf_op jit(solution)/shard_map/while/body/eval_jaxpr/ppermute | solution.py:14
  51.6 6.8 %collective-permute-start.1 = (f32[128,256]{1,0:T(8,128)S(1)}, f32[128,256]{1,0:T(8,128)S(1)}, u32[]{:S(2)}, u32[]{:S(2)}) collective-permute-start(f32[128,256]{1,0:T(8,128)S(1)} %convolution_add_fusion.3), channel_id=1, source_target_pairs={{28,0},{0,4},{4,8},{8,12},{12,16},{16,20},{20,24},{24,28},{29,1},{... | collective-permute-start | bytes 393224 | tf_op jit(solution)/shard_map/while/body/eval_jaxpr/ppermute | solution.py:14
  58.4 7.5 %collective-permute-start = (bf16[128,768]{1,0:T(8,128)(2,1)S(1)}, bf16[128,768]{1,0:T(8,128)(2,1)S(1)}, u32[]{:S(2)}, u32[]{:S(2)}) collective-permute-start(bf16[128,768]{1,0:T(8,128)(2,1)S(1)} %copy.17), channel_id=1, source_target_pairs={{28,0},{0,4},{4,8},{8,12},{12,16},{16,20},{20,24},{24,28},{29,1},{... | collective-permute-start | bytes 589832 | tf_op jit(solution)/shard_map/while/body/eval_jaxpr/ppermute | solution.py:14
  59.1 6.8 %collective-permute-start.1 = (f32[128,256]{1,0:T(8,128)S(1)}, f32[128,256]{1,0:T(8,128)S(1)}, u32[]{:S(2)}, u32[]{:S(2)}) collective-permute-start(f32[128,256]{1,0:T(8,128)S(1)} %convolution_add_fusion.3), channel_id=1, source_target_pairs={{28,0},{0,4},{4,8},{8,12},{12,16},{16,20},{20,24},{24,28},{29,1},{... | collective-permute-start | bytes 393224 | tf_op jit(solution)/shard_map/while/body/eval_jaxpr/ppermute | solution.py:14
  65.9 6.6 %copy-start.1 = (f32[256,256]{1,0:T(8,128)S(1)}, f32[256,256]{1,0:T(8,128)}, u32[]{:S(2)}) copy-start(f32[256,256]{1,0:T(8,128)} %param.11) | copy-start | bytes 786436
  66.4 5.3 %collective-permute-start.2 = (f32[128,256]{1,0:T(8,128)S(1)}, f32[128,256]{1,0:T(8,128)S(1)}, u32[]{:S(2)}, u32[]{:S(2)}) collective-permute-start(f32[128,256]{1,0:T(8,128)S(1)} %convolution_add_fusion.1), channel_id=1, source_target_pairs={{28,0},{0,4},{4,8},{8,12},{12,16},{16,20},{20,24},{24,28},{29,1},{... | collective-permute-start | bytes 393224 | tf_op jit(solution)/shard_map/ppermute | solution.py:14
  71.8 0.7 copy-start.4
  72.4 176.6 %all-reduce.5.cloned.1.call-start = ((), (), s32[]{:S(2)}) async-start(), calls=%async_computation.1 | async-start | bytes 262144 | tf_op jit(solution)/shard_map/psum | solution.py:86
  123.1 126.0 %copy-start.6 = (f32[128]{0:T(128)S(1)}, f32[128]{0:T(128)}, u32[]{:S(2)}) copy-start(f32[128]{0:T(128)} %param.17) | copy-start | bytes 1540
  254.6 8.9 %copy-start.2 = (f32[128,256]{1,0:T(8,128)S(1)}, f32[128,256]{1,0:T(8,128)}, u32[]{:S(2)}) copy-start(f32[128,256]{1,0:T(8,128)} %param.14) | copy-start | bytes 393220
Sparse Core Ops, SparseCore 0:
  72.6 35.7 all-reduce.2
  125.8 123.2 all-reduce.4
where the time goes:
time: 271 us
  waiting for transfers between devices  206 us (76%)
  other arithmetic  15 us (6%)
  between operations  14.3 us (5%)
  blocking collectives  9.79 us (4%)
  local copies, waits for them, and re-layouts  9.77 us (4%)
  matrix products  9.7 us (4%)
  starting transfers between devices  5.97 us (2%)
    psum x1, waiting for transfers between devices, local(): projected = lax.psum(local_proj, ('blk', 'col'))  123 us
    ppermute x15, waiting for transfers between devices, shifted(): return lax.ppermute(block, axis, route)  48.3 us
    psum x1, waiting for transfers between devices, local(): prediction = lax.psum(partial_value, 'col')  35 us
    all_gather x1, blocking collectives, local(): lax.all_gather(residual_full.astype(jnp.bfloat16), 'blk', axis=0, tiled=T...  9.79 us
    scatter-add x1, other arithmetic, local(): adjusted = gradient.at[position].add(-correction, mode='drop')  8.88 us
    ppermute x15, starting transfers between devices, shifted(): return lax.ppermute(block, axis, route)  5.89 us
  transfers between devices with their start and end apart: 17, of which 10 were waited for; matrix products, arithmetic and copies ran while one was open for 2% of the time, Pallas kernels for 0%

commit v1 on v0

--- a/solution.py
+++ b/solution.py
@@ -83,7 +83,8 @@
     picked = jnp.where(inside[:, None], jnp.take(gradient, target_row, axis=0), 0.0)
     highest = lax.Precision.HIGHEST
     local_proj = lax.dot_general(eigvecs, picked, (((0,), (0,)), ((), ())), precision=highest)
-    projected = lax.psum(local_proj, ("blk", "col"))
+    partial = lax.psum(local_proj, "col")
+    projected = lax.psum(partial, "blk")
     correction = jnp.dot(eigvecs, coefficient[:, None] * projected, precision=highest)
     adjusted = gradient.at[position].add(-correction, mode="drop")
     return (own_resid, weights - step_size * adjusted)

time: 271 us -> 237 us (0.87)
  waiting for transfers between devices: 206 us -> 172 us
    psum x1 -> x2, waiting for transfers between devices: 123 us -> 89.1 us  [the longest x1 55.5 us: local(): projected = lax.psum(partial, 'blk')]
  transfers between devices with their start and end apart: 17 -> 18, of which waited for: 10 -> 11; matrix products, arithmetic and copies ran while one was open for 2% -> 2% of each run, Pallas kernels for 0% -> 0%
where the time goes in v1:
time: 237 us
  waiting for transfers between devices  172 us (73%)
  other arithmetic  15 us (6%)
  between operations  14 us (6%)
  blocking collectives  9.79 us (4%)
  local copies, waits for them, and re-layouts  9.77 us (4%)
  matrix products  9.69 us (4%)
  starting transfers between devices  6.01 us (3%)
    psum x1, waiting for transfers between devices, local(): projected = lax.psum(partial, 'blk')  55.5 us
    ppermute x15, waiting for transfers between devices, shifted(): return lax.ppermute(block, axis, route)  48.4 us
    psum x1, waiting for transfers between devices, local(): prediction = lax.psum(partial_value, 'col')  35 us
    psum x1, waiting for transfers between devices, local(): partial = lax.psum(local_proj, 'col')  33.5 us
    all_gather x1, blocking collectives, local(): lax.all_gather(residual_full.astype(jnp.bfloat16), 'blk', axis=0, tiled=T...  9.79 us
    scatter-add x1, other arithmetic, local(): adjusted = gradient.at[position].add(-correction, mode='drop')  8.88 us
    ppermute x15, starting transfers between devices, shifted(): return lax.ppermute(block, axis, route)  5.88 us
  transfers between devices with their start and end apart: 18, of which 11 were waited for; matrix products, arithmetic and copies ran while one was open for 2% of the time, Pallas kernels for 0%

profile of v1, /device:TPU:0, one launch (start us, length us, event | category | flops | bytes accessed | tf_op | source)
XLA Modules:
  0.0 237.0 jit_solution(137709659229433875)
XLA Ops:
  7.2 0.8 compare_and_fusion.2
  8.0 0.7 compare_select_fusion.2
  8.7 1.0 multiply_reduce_fusion.2
  9.7 0.9 convert_element_type.36
  10.6 2.0 gather_fusion
  12.8 53.1 %while.19 = (s32[]{:T(128)}, bf16[128,768]{1,0:T(8,128)(2,1)S(1)}, f32[128,256]{1,0:T(8,128)S(1)}, bf16[1024,128]{1,0:T(8,128)(2,1)S(1)}, f32[128]{0:T(128)S(1)}...) while((s32[]{:T(128)}, bf16[128,768]{1,0:T(8,128)(2,1)S(1)}, ...), condition=%wide.region_3.4_spmd, body=%wide.region_1.3_spmd.sunk | while | flops 33980304 | bytes 2721664 | solution.py:63
  12.9 0.5 collective-permute-start
  13.5 0.3 constant_dynamic-update-slice_fusion.3
  13.8 0.2 convolution_add_fusion.3
  14.0 2.6 %collective-permute-start.1 = (f32[128,256]{1,0:T(8,128)S(1)}, f32[128,256]{1,0:T(8,128)S(1)}, u32[]{:S(2)}, u32[]{:S(2)}) collective-permute-start(f32[128,256]{1,0:T(8,128)S(1)} %convolution_add_fusion.3), channel_id=1, source_target_pairs={{28,0},{0,4},{4,8},{8,12},{12,16},{16,20},{20,24},{24,28},{29,1},{... | collective-permute-start | bytes 393224 | tf_op jit(solution)/shard_map/while/body/eval_jaxpr/ppermute | solution.py:14
  16.6 4.4 %collective-permute-done.1 = f32[128,256]{1,0:T(8,128)S(1)} collective-permute-done((f32[128,256]{1,0:T(8,128)S(1)}, f32[128,256]{1,0:T(8,128)S(1)}, u32[]{:S(2)}, u32[]{:S(2)}) %collective-permute-start.1) | collective-permute-done | bytes 131104 | tf_op jit(solution)/shard_map/while/body/eval_jaxpr/ppermute | solution.py:14
  21.3 0.3 constant_dynamic-update-slice_fusion.3
  21.5 0.2 convolution_add_fusion.3
  21.7 1.5 collective-permute-start.1
  23.2 5.3 %collective-permute-done.1 = f32[128,256]{1,0:T(8,128)S(1)} collective-permute-done((f32[128,256]{1,0:T(8,128)S(1)}, f32[128,256]{1,0:T(8,128)S(1)}, u32[]{:S(2)}, u32[]{:S(2)}) %collective-permute-start.1) | collective-permute-done | bytes 131104 | tf_op jit(solution)/shard_map/while/body/eval_jaxpr/ppermute | solution.py:14
  28.7 0.3 constant_dynamic-update-slice_fusion.3
  29.0 0.2 convolution_add_fusion.3
  29.2 0.6 collective-permute-start.1
  29.7 6.2 %collective-permute-done.1 = f32[128,256]{1,0:T(8,128)S(1)} collective-permute-done((f32[128,256]{1,0:T(8,128)S(1)}, f32[128,256]{1,0:T(8,128)S(1)}, u32[]{:S(2)}, u32[]{:S(2)}) %collective-permute-start.1) | collective-permute-done | bytes 131104 | tf_op jit(solution)/shard_map/while/body/eval_jaxpr/ppermute | solution.py:14
  36.2 0.3 constant_dynamic-update-slice_fusion.3
  36.5 0.2 convolution_add_fusion.3
  36.7 6.8 %collective-permute-done.1 = f32[128,256]{1,0:T(8,128)S(1)} collective-permute-done((f32[128,256]{1,0:T(8,128)S(1)}, f32[128,256]{1,0:T(8,128)S(1)}, u32[]{:S(2)}, u32[]{:S(2)}) %collective-permute-start.1) | collective-permute-done | bytes 131104 | tf_op jit(solution)/shard_map/while/body/eval_jaxpr/ppermute | solution.py:14
  43.7 0.3 constant_dynamic-update-slice_fusion.3
  44.0 0.2 convolution_add_fusion.3
  44.2 6.8 %collective-permute-done.1 = f32[128,256]{1,0:T(8,128)S(1)} collective-permute-done((f32[128,256]{1,0:T(8,128)S(1)}, f32[128,256]{1,0:T(8,128)S(1)}, u32[]{:S(2)}, u32[]{:S(2)}) %collective-permute-start.1) | collective-permute-done | bytes 131104 | tf_op jit(solution)/shard_map/while/body/eval_jaxpr/ppermute | solution.py:14
  51.2 0.3 constant_dynamic-update-slice_fusion.3
  51.4 0.2 convolution_add_fusion.3
  51.7 6.8 %collective-permute-done.1 = f32[128,256]{1,0:T(8,128)S(1)} collective-permute-done((f32[128,256]{1,0:T(8,128)S(1)}, f32[128,256]{1,0:T(8,128)S(1)}, u32[]{:S(2)}, u32[]{:S(2)}) %collective-permute-start.1) | collective-permute-done | bytes 131104 | tf_op jit(solution)/shard_map/while/body/eval_jaxpr/ppermute | solution.py:14
  58.6 0.3 constant_dynamic-update-slice_fusion.3
  59.1 6.8 %collective-permute-done.1 = f32[128,256]{1,0:T(8,128)S(1)} collective-permute-done((f32[128,256]{1,0:T(8,128)S(1)}, f32[128,256]{1,0:T(8,128)S(1)}, u32[]{:S(2)}, u32[]{:S(2)}) %collective-permute-start.1) | collective-permute-done | bytes 131104 | tf_op jit(solution)/shard_map/while/body/eval_jaxpr/ppermute | solution.py:14
  66.0 0.3 constant_dynamic-update-slice_fusion.1
  66.3 0.2 convolution_add_fusion.1
  66.5 5.3 %collective-permute-done.2 = f32[128,256]{1,0:T(8,128)S(1)} collective-permute-done((f32[128,256]{1,0:T(8,128)S(1)}, f32[128,256]{1,0:T(8,128)S(1)}, u32[]{:S(2)}, u32[]{:S(2)}) %collective-permute-start.2) | collective-permute-done | bytes 131104 | tf_op jit(solution)/shard_map/ppermute | solution.py:14
  71.8 0.7 copy-done.4
  72.5 0.8 gather_fusion.1
  73.3 35.0 %all-reduce.4.cloned.1.call-done = f32[128,256]{1,0:T(8,128)} async-done(((f32[128,256]{1,0:T(8,128)}), f32[128,256]{1,0:T(8,128)}) %all-reduce.4.cloned.1.call-update) | async-done | bytes 131088 | tf_op jit(solution)/shard_map/psum | solution.py:69
  108.3 1.0 fusion.27
  109.3 9.8 %all_gather.3 = bf16[1024,256]{1,0:T(8,128)(2,1)S(1)} all-gather(bf16[128,256]{1,0:T(8,128)(2,1)S(1)} %get-tuple-element.224), channel_id=1, replica_groups=mesh['blk'=8,'col'=4] {'blk'}, dimensions={0}, use_global_device_ids=true | all-gather | bytes 589824 | tf_op jit(solution)/shard_map/all_gather | solution.py:71
  119.1 0.3 fusion.28
  119.4 3.7 %gather_fusion.2 = f32[1536,256]{1,0:T(8,128)S(1)} fusion(f32[128,256]{1,0:T(8,128)S(1)} %fusion.28, s32[2048]{0:T(1024)S(1)} %pad_clamp_fusion), kind=kCustom, calls=%fused_computation.2 | custom fusion | bytes 3151872 | tf_op jit(solution)/shard_map/jit(_take)/gather | solution.py:83
  123.1 2.6 %fusion.10 = f32[128,256]{1,0:T(8,128)} fusion(f32[1536,128]{1,0:T(8,128)S(1)} %copy-done, f32[1536,256]{1,0:T(8,128)S(1)} %gather_fusion.2, pred[1536]{0:T(1024)(128)(4,1)S(1)} %get-tuple-element.222, pred[1536]{0:T(1024)(128)(4,1)S(1)} %get-tuple-element.228), kind=kOutput, calls=%fused_computation.19 | convolution fusion | flops 604766208 | bytes 2493440 | tf_op jit(solution)/shard_map/dot_general | solution.py:85
  125.7 33.5 %all-reduce.6.cloned.1.call-done = f32[128,256]{1,0:T(8,128)} async-done(((f32[128,256]{1,0:T(8,128)}), f32[128,256]{1,0:T(8,128)}) %all-reduce.6.cloned.1.call-update) | async-done | bytes 131088 | tf_op jit(solution)/shard_map/psum | solution.py:86
  159.3 0.6 constant_dynamic-slice_fusion
  159.9 55.5 %all-reduce.8.cloned.1.call-done = f32[128,256]{1,0:T(8,128)} async-done(((f32[128,256]{1,0:T(8,128)}), f32[128,256]{1,0:T(8,128)}) %all-reduce.8.cloned.1.call-update) | async-done | bytes 131088 | tf_op jit(solution)/shard_map/psum | solution.py:87
  215.5 3.6 %fusion.6 = f32[1536,256]{0,1:T(8,128)} fusion(f32[1536,128]{1,0:T(8,128)S(1)} %copy-done, f32[128,256]{1,0:T(8,128)} %all-reduce.8.cloned.1.call-done, f32[128]{0:T(128)S(1)} %copy-done.6), kind=kOutput, calls=%fused_computation.15 | convolution fusion | flops 604405760 | bytes 2490880 | tf_op jit(solution)/shard_map/dot_general | solution.py:88
  219.0 1.9 copy.10
  220.9 8.9 %scatter_fusion = f32[128,256]{1,0:T(8,128)S(1)} fusion(f32[128,256]{1,0:T(8,128)S(1)} %fusion.28, s32[1536]{0:T(1024)S(1)} %compare_select_fusion.1, f32[1536,256]{1,0:T(8,128)S(1)} %copy.10), kind=kCustom, calls=%fused_computation.3 | custom fusion | flops 393216 | bytes 4724736 | tf_op jit(solution)/shard_map/scatter-add | solution.py:89
  229.8 0.7 multiply_subtract_fusion
  (60 shorter events, 2.3 us)
Async XLA Ops:
  7.2 115.9 %copy-start = (f32[1536,128]{1,0:T(8,128)S(1)}, f32[1536,128]{1,0:T(8,128)}, u32[]{:S(2)}) copy-start(f32[1536,128]{1,0:T(8,128)} %param.16) | copy-start | bytes 2359300
  7.2 5.6 %copy-start.3 = (bf16[128,768]{1,0:T(8,128)(2,1)S(1)}, bf16[128,768]{1,0:T(8,128)(2,1)}, u32[]{:S(2)}) copy-start(bf16[128,768]{1,0:T(8,128)(2,1)} %param.13) | copy-start | bytes 589828
  7.2 101.1 %all-reduce.4.cloned.1.call-start = ((), (), s32[]{:S(2)}) async-start(), calls=%async_computation | async-start | bytes 262144 | tf_op jit(solution)/shard_map/psum | solution.py:69
  12.8 59.7 %copy-start.5 = (s32[1536]{0:T(1024)S(1)}, s32[1536]{0:T(1024)}, u32[]{:S(2)}) copy-start(s32[1536]{0:T(1024)} %param.15) | copy-start | bytes 18436
  12.9 8.2 %collective-permute-start = (bf16[128,768]{1,0:T(8,128)(2,1)S(1)}, bf16[128,768]{1,0:T(8,128)(2,1)S(1)}, u32[]{:S(2)}, u32[]{:S(2)}) collective-permute-start(bf16[128,768]{1,0:T(8,128)(2,1)S(1)} %copy.17), channel_id=1, source_target_pairs={{28,0},{0,4},{4,8},{8,12},{12,16},{16,20},{20,24},{24,28},{29,1},{... | collective-permute-start | bytes 589832 | tf_op jit(solution)/shard_map/while/body/eval_jaxpr/ppermute | solution.py:14
  14.0 7.1 %collective-permute-start.1 = (f32[128,256]{1,0:T(8,128)S(1)}, f32[128,256]{1,0:T(8,128)S(1)}, u32[]{:S(2)}, u32[]{:S(2)}) collective-permute-start(f32[128,256]{1,0:T(8,128)S(1)} %convolution_add_fusion.3), channel_id=1, source_target_pairs={{28,0},{0,4},{4,8},{8,12},{12,16},{16,20},{20,24},{24,28},{29,1},{... | collective-permute-start | bytes 393224 | tf_op jit(solution)/shard_map/while/body/eval_jaxpr/ppermute | solution.py:14
  21.1 7.5 %collective-permute-start = (bf16[128,768]{1,0:T(8,128)(2,1)S(1)}, bf16[128,768]{1,0:T(8,128)(2,1)S(1)}, u32[]{:S(2)}, u32[]{:S(2)}) collective-permute-start(bf16[128,768]{1,0:T(8,128)(2,1)S(1)} %copy.17), channel_id=1, source_target_pairs={{28,0},{0,4},{4,8},{8,12},{12,16},{16,20},{20,24},{24,28},{29,1},{... | collective-permute-start | bytes 589832 | tf_op jit(solution)/shard_map/while/body/eval_jaxpr/ppermute | solution.py:14
  21.7 6.8 %collective-permute-start.1 = (f32[128,256]{1,0:T(8,128)S(1)}, f32[128,256]{1,0:T(8,128)S(1)}, u32[]{:S(2)}, u32[]{:S(2)}) collective-permute-start(f32[128,256]{1,0:T(8,128)S(1)} %convolution_add_fusion.3), channel_id=1, source_target_pairs={{28,0},{0,4},{4,8},{8,12},{12,16},{16,20},{20,24},{24,28},{29,1},{... | collective-permute-start | bytes 393224 | tf_op jit(solution)/shard_map/while/body/eval_jaxpr/ppermute | solution.py:14
  28.5 7.5 %collective-permute-start = (bf16[128,768]{1,0:T(8,128)(2,1)S(1)}, bf16[128,768]{1,0:T(8,128)(2,1)S(1)}, u32[]{:S(2)}, u32[]{:S(2)}) collective-permute-start(bf16[128,768]{1,0:T(8,128)(2,1)S(1)} %copy.17), channel_id=1, source_target_pairs={{28,0},{0,4},{4,8},{8,12},{12,16},{16,20},{20,24},{24,28},{29,1},{... | collective-permute-start | bytes 589832 | tf_op jit(solution)/shard_map/while/body/eval_jaxpr/ppermute | solution.py:14
  29.2 6.8 %collective-permute-start.1 = (f32[128,256]{1,0:T(8,128)S(1)}, f32[128,256]{1,0:T(8,128)S(1)}, u32[]{:S(2)}, u32[]{:S(2)}) collective-permute-start(f32[128,256]{1,0:T(8,128)S(1)} %convolution_add_fusion.3), channel_id=1, source_target_pairs={{28,0},{0,4},{4,8},{8,12},{12,16},{16,20},{20,24},{24,28},{29,1},{... | collective-permute-start | bytes 393224 | tf_op jit(solution)/shard_map/while/body/eval_jaxpr/ppermute | solution.py:14
  36.0 7.5 %collective-permute-start = (bf16[128,768]{1,0:T(8,128)(2,1)S(1)}, bf16[128,768]{1,0:T(8,128)(2,1)S(1)}, u32[]{:S(2)}, u32[]{:S(2)}) collective-permute-start(bf16[128,768]{1,0:T(8,128)(2,1)S(1)} %copy.17), channel_id=1, source_target_pairs={{28,0},{0,4},{4,8},{8,12},{12,16},{16,20},{20,24},{24,28},{29,1},{... | collective-permute-start | bytes 589832 | tf_op jit(solution)/shard_map/while/body/eval_jaxpr/ppermute | solution.py:14
  36.6 6.8 %collective-permute-start.1 = (f32[128,256]{1,0:T(8,128)S(1)}, f32[128,256]{1,0:T(8,128)S(1)}, u32[]{:S(2)}, u32[]{:S(2)}) collective-permute-start(f32[128,256]{1,0:T(8,128)S(1)} %convolution_add_fusion.3), channel_id=1, source_target_pairs={{28,0},{0,4},{4,8},{8,12},{12,16},{16,20},{20,24},{24,28},{29,1},{... | collective-permute-start | bytes 393224 | tf_op jit(solution)/shard_map/while/body/eval_jaxpr/ppermute | solution.py:14
  43.5 7.5 %collective-permute-start = (bf16[128,768]{1,0:T(8,128)(2,1)S(1)}, bf16[128,768]{1,0:T(8,128)(2,1)S(1)}, u32[]{:S(2)}, u32[]{:S(2)}) collective-permute-start(bf16[128,768]{1,0:T(8,128)(2,1)S(1)} %copy.17), channel_id=1, source_target_pairs={{28,0},{0,4},{4,8},{8,12},{12,16},{16,20},{20,24},{24,28},{29,1},{... | collective-permute-start | bytes 589832 | tf_op jit(solution)/shard_map/while/body/eval_jaxpr/ppermute | solution.py:14
  44.1 6.8 %collective-permute-start.1 = (f32[128,256]{1,0:T(8,128)S(1)}, f32[128,256]{1,0:T(8,128)S(1)}, u32[]{:S(2)}, u32[]{:S(2)}) collective-permute-start(f32[128,256]{1,0:T(8,128)S(1)} %convolution_add_fusion.3), channel_id=1, source_target_pairs={{28,0},{0,4},{4,8},{8,12},{12,16},{16,20},{20,24},{24,28},{29,1},{... | collective-permute-start | bytes 393224 | tf_op jit(solution)/shard_map/while/body/eval_jaxpr/ppermute | solution.py:14
  51.0 7.5 %collective-permute-start = (bf16[128,768]{1,0:T(8,128)(2,1)S(1)}, bf16[128,768]{1,0:T(8,128)(2,1)S(1)}, u32[]{:S(2)}, u32[]{:S(2)}) collective-permute-start(bf16[128,768]{1,0:T(8,128)(2,1)S(1)} %copy.17), channel_id=1, source_target_pairs={{28,0},{0,4},{4,8},{8,12},{12,16},{16,20},{20,24},{24,28},{29,1},{... | collective-permute-start | bytes 589832 | tf_op jit(solution)/shard_map/while/body/eval_jaxpr/ppermute | solution.py:14
  51.6 6.8 %collective-permute-start.1 = (f32[128,256]{1,0:T(8,128)S(1)}, f32[128,256]{1,0:T(8,128)S(1)}, u32[]{:S(2)}, u32[]{:S(2)}) collective-permute-start(f32[128,256]{1,0:T(8,128)S(1)} %convolution_add_fusion.3), channel_id=1, source_target_pairs={{28,0},{0,4},{4,8},{8,12},{12,16},{16,20},{20,24},{24,28},{29,1},{... | collective-permute-start | bytes 393224 | tf_op jit(solution)/shard_map/while/body/eval_jaxpr/ppermute | solution.py:14
  58.4 7.5 %collective-permute-start = (bf16[128,768]{1,0:T(8,128)(2,1)S(1)}, bf16[128,768]{1,0:T(8,128)(2,1)S(1)}, u32[]{:S(2)}, u32[]{:S(2)}) collective-permute-start(bf16[128,768]{1,0:T(8,128)(2,1)S(1)} %copy.17), channel_id=1, source_target_pairs={{28,0},{0,4},{4,8},{8,12},{12,16},{16,20},{20,24},{24,28},{29,1},{... | collective-permute-start | bytes 589832 | tf_op jit(solution)/shard_map/while/body/eval_jaxpr/ppermute | solution.py:14
  59.1 6.8 %collective-permute-start.1 = (f32[128,256]{1,0:T(8,128)S(1)}, f32[128,256]{1,0:T(8,128)S(1)}, u32[]{:S(2)}, u32[]{:S(2)}) collective-permute-start(f32[128,256]{1,0:T(8,128)S(1)} %convolution_add_fusion.3), channel_id=1, source_target_pairs={{28,0},{0,4},{4,8},{8,12},{12,16},{16,20},{20,24},{24,28},{29,1},{... | collective-permute-start | bytes 393224 | tf_op jit(solution)/shard_map/while/body/eval_jaxpr/ppermute | solution.py:14
  65.9 6.7 %copy-start.1 = (f32[256,256]{1,0:T(8,128)S(1)}, f32[256,256]{1,0:T(8,128)}, u32[]{:S(2)}) copy-start(f32[256,256]{1,0:T(8,128)} %param.11) | copy-start | bytes 786436
  66.4 5.3 %collective-permute-start.2 = (f32[128,256]{1,0:T(8,128)S(1)}, f32[128,256]{1,0:T(8,128)S(1)}, u32[]{:S(2)}, u32[]{:S(2)}) collective-permute-start(f32[128,256]{1,0:T(8,128)S(1)} %convolution_add_fusion.1), channel_id=1, source_target_pairs={{28,0},{0,4},{4,8},{8,12},{12,16},{16,20},{20,24},{24,28},{29,1},{... | collective-permute-start | bytes 393224 | tf_op jit(solution)/shard_map/ppermute | solution.py:14
  71.8 0.7 copy-start.4
  72.4 86.8 %all-reduce.6.cloned.1.call-start = ((), (), s32[]{:S(2)}) async-start(), calls=%async_computation.1 | async-start | bytes 262144 | tf_op jit(solution)/shard_map/psum | solution.py:86
  123.1 92.4 %copy-start.6 = (f32[128]{0:T(128)S(1)}, f32[128]{0:T(128)}, u32[]{:S(2)}) copy-start(f32[128]{0:T(128)} %param.17) | copy-start | bytes 1540
  125.7 89.8 %all-reduce.8.cloned.1.call-start = ((), (), s32[]{:S(2)}) async-start(), calls=%async_computation.2 | async-start | bytes 262144 | tf_op jit(solution)/shard_map/psum | solution.py:87
  220.9 8.9 %copy-start.2 = (f32[128,256]{1,0:T(8,128)S(1)}, f32[128,256]{1,0:T(8,128)}, u32[]{:S(2)}) copy-start(f32[128,256]{1,0:T(8,128)} %param.14) | copy-start | bytes 393220
Sparse Core Ops, SparseCore 0:
  72.6 35.7 all-reduce.3
  125.8 33.4 all-reduce.5
  162.3 53.0 all-reduce.7
